TPU v7x, 32 devices: a whole 2x2x4 slice. The times are simulated.
32 devices in a mesh: ya: 8 (over z, y), zb: 4 (over x, core).
Axes of the slice: x: 2, y: 2, z: 4, core: 2. Of those that a mesh axis runs over, the one named last changes fastest.
Arguments:
- source: float32 [128, 128, 512], P(None, 'ya', 'zb'), may hold values from -6 to 6
- symbol_x: float32 [128], replicated, may hold values from 0.3 to 3
- symbol_y: float32 [128], replicated, may hold values from 0.3 to 3
- symbol_z: float32 [512], replicated, may hold values from 0.3 to 3
Outputs:
- modes: float32 [128, 128, 512], P('ya', 'zb')
All inputs are finite; a program needn't handle non-finite values.
Results may differ from a plain program's by a relative error of at most 0.000071.
Values sent between devices are 32-bit elements; how exact they have to be, the bound alone decides.
A program may use at most 64 MiB of HBM per device.

v0:
```python
import jax
import jax.numpy as jnp
from jax import lax
from jax.sharding import PartitionSpec as P


def transform_table(count):
    rank = jnp.arange(count)
    angle = (
        jnp.pi
        / (count + 1)
        * ((rank[:, None] + 1) * (rank[None, :] + 1) % (2 * count + 2)).astype(jnp.float32)
    )
    return jnp.sin(angle) * (2.0 / (count + 1)) ** 0.5


def transform_dim(values, dim):
    moved = jnp.tensordot(
        values,
        transform_table(values.shape[dim]),
        axes=([dim], [0]),
        precision=lax.Precision.HIGHEST,
    )
    return jnp.moveaxis(moved, -1, dim)


def body(source, symbol_x, symbol_y, symbol_z):
    part_values = source
    part_values = transform_dim(part_values, 0)
    part_values = lax.all_to_all(part_values, "ya", split_axis=0, concat_axis=1, tiled=True)
    part_values = transform_dim(part_values, 1)
    pencil_values = part_values
    pencil_values = lax.all_to_all(pencil_values, "zb", split_axis=1, concat_axis=2, tiled=True)
    pencil_values = transform_dim(pencil_values, 2)
    share_x = pencil_values.shape[0]
    part_x = lax.dynamic_slice_in_dim(symbol_x, lax.axis_index("ya") * share_x, share_x)
    share_y = pencil_values.shape[1]
    part_y = lax.dynamic_slice_in_dim(symbol_y, lax.axis_index("zb") * share_y, share_y)
    symbol = part_x[:, None, None] + part_y[None, :, None] + symbol_z[None, None, :]
    pencil_values = pencil_values * lax.rsqrt(symbol)
    return pencil_values


def solution(mesh):
    placed = (P(None, "ya", "zb"), P(), P(), P())
    return jax.shard_map(
        body, mesh=mesh, in_specs=placed, out_specs=P("ya", "zb", None), check_vma=False
    )
```

profile of v0, /device:TPU:0, one launch (start us, length us, event | category | flops | bytes accessed | tf_op | source)
XLA Modules:
  0.0 66.0 jit_solution(8343601692508259223)
XLA Ops:
  0.0 0.0 copy-start
  0.0 1.2 %copy-done = f32[128,16,128]{2,1,0:T(8,128)S(1)} copy-done((f32[128,16,128]{2,1,0:T(8,128)S(1)}, f32[128,16,128]{2,1,0:T(8,128)}, u32[]{:S(2)}) %copy-start) | copy-done | bytes 1048600
  1.2 1.6 %fusion.6 = f32[128,16,128]{2,0,1:T(8,128)S(1)} fusion(f32[128,16,128]{2,1,0:T(8,128)S(1)} %copy-done, s32[128]{0:T(128)S(1)} %iota_add_fusion.1), kind=kOutput, calls=%fused_computation.8 | convolution fusion | flops 402817024 | bytes 2097664 | tf_op jit(solution)/shard_map/dot_general | solution.py:18
  2.8 0.6 copy.24
  3.5 32.9 %all_to_all.36 = f32[128,16,128]{2,1,0:T(8,128)S(1)} all-to-all(f32[128,16,128]{2,1,0:T(8,128)S(1)} %copy.24), channel_id=1, replica_groups=mesh['ya'=8,'zb'=4] {'ya'}, dimensions={0} | all-to-all | bytes 2097152 | tf_op jit(solution)/shard_map/all_to_all | solution.py:30
  36.3 0.1 copy.25
  36.4 2.0 %convolution_bitcast_fusion = f32[16,128,128]{1,2,0:T(8,128)S(1)} fusion(f32[16,128,128]{2,1,0:T(8,128)S(1)} %bitcast.21, s32[128]{0:T(128)S(1)} %iota_add_fusion.1), kind=kOutput, calls=%fused_computation.2 | convolution fusion | flops 402817024 | bytes 2097664 | tf_op jit(solution)/shard_map/dot_general | solution.py:18
  38.4 1.4 %copy.27 = f32[16,128,128]{2,0,1:T(8,128)} copy(f32[16,128,128]{1,2,0:T(8,128)S(1)} %convolution_bitcast_fusion) | data formatting | bytes 2097152 | tf_op jit(solution)/shard_map/transpose | solution.py:24
  39.8 3.7 %all-to-all-start.1 = ((f32[16,128,128]{2,0,1:T(8,128)}), f32[16,128,128]{2,0,1:T(8,128)S(1)}, u32[]{:S(2)}, u32[]{:S(2)}) async-start(f32[16,128,128]{2,0,1:T(8,128)} %copy.27), calls=%async_computation.1 | async-start | bytes 2097152 | tf_op jit(solution)/shard_map/all_to_all | solution.py:33
  43.5 0.0 copy-start.2
  43.5 0.6 copy-done.2
  44.2 0.1 dynamic_slice.7
  44.2 0.0 copy-start.3
  44.2 0.7 copy-done.3
  44.9 0.1 dynamic_slice.6
  45.0 0.1 broadcast_add_fusion
  45.0 12.7 %all-to-all-done.1 = f32[16,128,128]{2,0,1:T(8,128)S(1)} async-done(((f32[16,128,128]{2,0,1:T(8,128)}), f32[16,128,128]{2,0,1:T(8,128)S(1)}, u32[]{:S(2)}, u32[]{:S(2)}) %all-to-all-start.1) | async-done | bytes 1048608 | tf_op jit(solution)/shard_map/all_to_all | solution.py:33
  57.7 0.7 %copy.29 = f32[16,32,4,128]{3,2,1,0:T(4,128)S(1)} copy(f32[16,32,4,128]{3,0,1,2:T(8,128)S(1)} %bitcast.19) | data formatting | bytes 2097152 | tf_op jit(solution)/shard_map/all_to_all | solution.py:33
  58.4 0.0 copy-start.1
  58.4 0.4 all_to_all.33
  58.8 0.2 copy-done.1
  59.1 6.9 %convolution_multiply_fusion = f32[16,32,512]{2,1,0:T(8,128)} fusion(f32[16,32,512]{2,1,0:T(8,128)S(1)} %all_to_all.33, f32[512]{0:T(512)S(1)} %copy-done.1, f32[16,32]{1,0:T(8,128)S(1)} %broadcast_add_fusion, s32[512]{0:T(512)S(1)} %iota_add_fusion), kind=kOutput, calls=%fused_computation.1 | convolution fusion | flops 1613758464 | bytes 2103296 | tf_op jit(solution)/shard_map/dot_general | solution.py:18
  (2 shorter events, 0.0 us)
Async XLA Ops:
  0.0 1.2 %copy-start = (f32[128,16,128]{2,1,0:T(8,128)S(1)}, f32[128,16,128]{2,1,0:T(8,128)}, u32[]{:S(2)}) copy-start(f32[128,16,128]{2,1,0:T(8,128)} %param.4) | copy-start | bytes 3145732
  39.8 17.9 %all-to-all-start.1 = ((f32[16,128,128]{2,0,1:T(8,128)}), f32[16,128,128]{2,0,1:T(8,128)S(1)}, u32[]{:S(2)}, u32[]{:S(2)}) async-start(f32[16,128,128]{2,0,1:T(8,128)} %copy.27), calls=%async_computation.1 | async-start | bytes 2097152 | tf_op jit(solution)/shard_map/all_to_all | solution.py:33
  43.5 0.7 copy-start.2
  44.2 0.7 copy-start.3
  58.4 0.7 %copy-start.1 = (f32[512]{0:T(512)S(1)}, f32[512]{0:T(512)}, u32[]{:S(2)}) copy-start(f32[512]{0:T(512)} %param.7) | copy-start | bytes 6148
where the time goes:
time: 66.3 us; the launch traced here: 66 us
  blocking collectives  32.9 us (50%)
  waiting for transfers between devices  12.7 us (19%)
  matrix products  10.5 us (16%)
  local copies, waits for them, and re-layouts  6.11 us (9%)
  starting transfers between devices  3.7 us (6%)
    all_to_all x1, blocking collectives, body(): lax.all_to_all(part_values, 'ya', split_axis=0, concat_axis=1, tiled=True)  32.9 us
    all_to_all x1, waiting for transfers between devices, body(): lax.all_to_all(pencil_values, 'zb', split_axis=1, concat_axis=2, tiled=True)  12.7 us
    dot_general x3, matrix products, transform_dim(): jnp.tensordot(values, transform_table(values.shape[dim]), axes=([dim], [0...  10.5 us
    all_to_all x1, starting transfers between devices, body(): lax.all_to_all(pencil_values, 'zb', split_axis=1, concat_axis=2, tiled=True)  3.7 us
    unnamed x8, local copies, waits for them, and re-layouts  2.77 us
    transpose x1, local copies, waits for them, and re-layouts, transform_dim(): return jnp.moveaxis(moved, -1, dim)  1.38 us
  transfers between devices with their start and end apart: 1, of which 1 were waited for; matrix products, arithmetic and copies ran while one was open for 0% of the time, Pallas kernels for 0%

commit v1 on v0

--- a/solution.py
+++ b/solution.py
@@ -25,12 +25,20 @@
 
 
 def body(source, symbol_x, symbol_y, symbol_z):
+
+    def unite_inputs(load):
+        known = lax.axis_size("zb")
+        front = jnp.split(load, known, axis=1)
+        q_next = jnp.stack(front)
+        upper = lax.all_to_all(q_next, split_axis=0, axis_name="zb", concat_axis=0)
+        return jnp.concatenate(upper, axis=2)
+
     part_values = source
     part_values = transform_dim(part_values, 0)
     part_values = lax.all_to_all(part_values, "ya", split_axis=0, concat_axis=1, tiled=True)
     part_values = transform_dim(part_values, 1)
     pencil_values = part_values
-    pencil_values = lax.all_to_all(pencil_values, "zb", split_axis=1, concat_axis=2, tiled=True)
+    pencil_values = unite_inputs(pencil_values)
     pencil_values = transform_dim(pencil_values, 2)
     share_x = pencil_values.shape[0]
     part_x = lax.dynamic_slice_in_dim(symbol_x, lax.axis_index("ya") * share_x, share_x)

time: 66.3 us -> 64.1 us (0.967)
  local copies, waits for them, and re-layouts: 6.11 us -> 3.48 us
  other arithmetic: 0.08 us -> 1.12 us
    transpose x1 -> x0, local copies, waits for them, and re-layouts: 1.38 us -> none  [transform_dim(): return jnp.moveaxis(moved, -1, dim)]
    all_to_all x2 -> x0, local copies, waits for them, and re-layouts: 1.1 us -> none  [body(): lax.all_to_all(pencil_values, 'zb', split_axis=1, concat_axis=2, tiled=True)]
    another operation x0 -> x1, other arithmetic: none -> 1.04 us  [unite_inputs(): q_next = jnp.stack(front)]
where the time goes in v1:
time: 64.1 us; the launch traced here: 63.8 us
  blocking collectives  32.9 us (51%)
  waiting for transfers between devices  12.9 us (20%)
  matrix products  9.9 us (15%)
  starting transfers between devices  3.52 us (5%)
  local copies, waits for them, and re-layouts  3.48 us (5%)
  other arithmetic  1.12 us (2%)
    all_to_all x1, blocking collectives, body(): lax.all_to_all(part_values, 'ya', split_axis=0, concat_axis=1, tiled=True)  32.9 us
    all_to_all x1, waiting for transfers between devices, unite_inputs(): upper = lax.all_to_all(q_next, split_axis=0, axis_name='zb', concat_axis=0)  12.9 us
    dot_general x3, matrix products, transform_dim(): jnp.tensordot(values, transform_table(values.shape[dim]), axes=([dim], [0...  9.9 us
    all_to_all x1, starting transfers between devices, unite_inputs(): upper = lax.all_to_all(q_next, split_axis=0, axis_name='zb', concat_axis=0)  3.52 us
    unnamed x8, local copies, waits for them, and re-layouts  2.53 us
  transfers between devices with their start and end apart: 1, of which 1 were waited for; matrix products, arithmetic and copies ran while one was open for 0% of the time, Pallas kernels for 0%

profile of v1, /device:TPU:0, one launch (start us, length us, event | category | flops | bytes accessed | tf_op | source)
XLA Modules:
  0.0 63.8 jit_solution(213104408088966404)
XLA Ops:
  0.0 0.0 copy-start
  0.0 1.2 %copy-done = f32[128,16,128]{2,1,0:T(8,128)S(1)} copy-done((f32[128,16,128]{2,1,0:T(8,128)S(1)}, f32[128,16,128]{2,1,0:T(8,128)}, u32[]{:S(2)}) %copy-start) | copy-done | bytes 1048600
  1.2 1.6 %fusion.8 = f32[128,16,128]{2,0,1:T(8,128)S(1)} fusion(f32[128,16,128]{2,1,0:T(8,128)S(1)} %copy-done, s32[128]{0:T(128)S(1)} %iota_add_fusion.1), kind=kOutput, calls=%fused_computation.11 | convolution fusion | flops 402817024 | bytes 2097664 | tf_op jit(solution)/shard_map/dot_general | solution.py:18
  2.8 0.6 copy.11
  3.4 32.9 %all_to_all.23 = f32[128,16,128]{2,1,0:T(8,128)S(1)} all-to-all(f32[128,16,128]{2,1,0:T(8,128)S(1)} %copy.11), channel_id=1, replica_groups=mesh['ya'=8,'zb'=4] {'ya'}, dimensions={0} | all-to-all | bytes 2097152 | tf_op jit(solution)/shard_map/all_to_all | solution.py:38
  36.3 0.1 copy.12
  36.4 1.4 %convolution_bitcast_fusion = f32[16,128,128]{2,1,0:T(8,128)S(1)} fusion(f32[16,128,128]{2,1,0:T(8,128)S(1)} %bitcast.31, s32[128]{0:T(128)S(1)} %iota_add_fusion.1), kind=kOutput, calls=%fused_computation.2 | convolution fusion | flops 402817024 | bytes 2097664 | tf_op jit(solution)/shard_map/dot_general | solution.py:18
  37.9 0.1 slice_bitcast_fusion.3
  38.0 1.0 %pad_maximum_fusion = f32[4,16,32,128]{3,2,1,0:T(8,128)} fusion(f32[1,16,32,128]{3,2,1,0:T(8,128)S(1)} %get-tuple-element.6, f32[1,16,32,128]{3,2,1,0:T(8,128)S(1)} %get-tuple-element.7, f32[1,16,32,128]{3,2,1,0:T(8,128)S(1)} %get-tuple-element.8, f32[1,16,32,128]{3,2,1,0:T(8,128)S(1)} %get-tuple-element.5), kind=kLoop, calls=%fused_computation.10 | loop fusion | flops 786432 | bytes 2097152 | tf_op jit(solution)/shard_map/stack | solution.py:32
  39.0 3.5 %all-to-all-start.1 = ((f32[4,16,32,128]{3,2,1,0:T(8,128)}), f32[4,16,32,128]{3,2,1,0:T(8,128)S(1)}, u32[]{:S(2)}, u32[]{:S(2)}) async-start(f32[4,16,32,128]{3,2,1,0:T(8,128)} %pad_maximum_fusion), calls=%async_computation.1 | async-start | bytes 2097152 | tf_op jit(solution)/shard_map/all_to_all | solution.py:33
  42.5 0.0 copy-start.2
  42.5 0.6 %copy-done.2 = f32[128]{0:T(128)S(1)} copy-done((f32[128]{0:T(128)S(1)}, f32[128]{0:T(128)}, u32[]{:S(2)}) %copy-start.2) | copy-done | bytes 536
  43.2 0.1 dynamic_slice.6
  43.3 0.0 copy-start.3
  43.3 0.7 %copy-done.3 = f32[128]{0:T(128)S(1)} copy-done((f32[128]{0:T(128)S(1)}, f32[128]{0:T(128)}, u32[]{:S(2)}) %copy-start.3) | copy-done | bytes 536
  43.9 0.1 dynamic_slice.7
  44.0 0.0 copy-start.1
  44.0 0.1 broadcast_add_fusion
  44.1 12.9 %all-to-all-done.1 = f32[4,16,32,128]{3,2,1,0:T(8,128)S(1)} async-done(((f32[4,16,32,128]{3,2,1,0:T(8,128)}), f32[4,16,32,128]{3,2,1,0:T(8,128)S(1)}, u32[]{:S(2)}, u32[]{:S(2)}) %all-to-all-start.1) | async-done | bytes 1048608 | tf_op jit(solution)/shard_map/all_to_all | solution.py:33
  56.9 0.0 copy-done.1
  56.9 6.9 %convolution_multiply_fusion = f32[16,32,512]{2,1,0:T(8,128)} fusion(f32[512]{0:T(512)S(1)} %copy-done.1, f32[16,32]{1,0:T(8,128)S(1)} %broadcast_add_fusion, s32[512]{0:T(512)S(1)} %iota_add_fusion, f32[4,16,32,128]{3,2,1,0:T(8,128)S(1)} %all-to-all-done.1), kind=kOutput, calls=%fused_computation.1 | convolution fusion | flops 1613758464 | bytes 2103296 | tf_op jit(solution)/shard_map/dot_general | solution.py:18
  (2 shorter events, 0.0 us)
Async XLA Ops:
  0.0 1.2 %copy-start = (f32[128,16,128]{2,1,0:T(8,128)S(1)}, f32[128,16,128]{2,1,0:T(8,128)}, u32[]{:S(2)}) copy-start(f32[128,16,128]{2,1,0:T(8,128)} %param.4) | copy-start | bytes 3145732
  39.0 17.9 %all-to-all-start.1 = ((f32[4,16,32,128]{3,2,1,0:T(8,128)}), f32[4,16,32,128]{3,2,1,0:T(8,128)S(1)}, u32[]{:S(2)}, u32[]{:S(2)}) async-start(f32[4,16,32,128]{3,2,1,0:T(8,128)} %pad_maximum_fusion), calls=%async_computation.1 | async-start | bytes 2097152 | tf_op jit(solution)/shard_map/all_to_all | solution.py:33
  42.5 0.7 %copy-start.2 = (f32[128]{0:T(128)S(1)}, f32[128]{0:T(128)}, u32[]{:S(2)}) copy-start(f32[128]{0:T(128)} %param.5) | copy-start | bytes 1540
  43.3 0.7 %copy-start.3 = (f32[128]{0:T(128)S(1)}, f32[128]{0:T(128)}, u32[]{:S(2)}) copy-start(f32[128]{0:T(128)} %param.6) | copy-start | bytes 1540
  44.0 12.9 %copy-start.1 = (f32[512]{0:T(512)S(1)}, f32[512]{0:T(512)}, u32[]{:S(2)}) copy-start(f32[512]{0:T(512)} %param.7) | copy-start | bytes 6148
